TPU v7x, 128 devices: a whole 4x4x4 slice. The times are simulated.
128 devices in a mesh: grp: 4 (over z), seq: 32 (over x, y, core).
Axes of the slice: x: 4, y: 4, z: 4, core: 2. Of those that a mesh axis runs over, the one named last changes fastest.
Arguments:
- latent: bfloat16 [4, 4096, 32, 256], P('grp', 'seq'), may hold values from -6 to 6
- up_key: bfloat16 [4, 128, 256], replicated, may hold values from -0.5 to 0.5
- up_value: bfloat16 [4, 128, 256], replicated, may hold values from -0.5 to 0.5
- queries: bfloat16 [8, 64, 128], replicated, may hold values from -240 to 240, as said below
- lengths: int32 [8], replicated, may hold values from 1 to 16384
- block_dest: int32 [4096], replicated, may hold values from 0 to 127, as said below
Outputs:
- decode_latent: bfloat16 [128, 4, 32, 32, 256], P(('grp', 'seq'))
- attended: float32 [8, 8192], replicated
Inputs may be any that keep to these rules, and one draw needn't show every extreme that they name: `block_dest`: each aligned run of 128 entries (the blocks of one seq index in the prefill layout) names every decode device exactly once. `queries`: the new token's query entries, real-valued.
All inputs are finite; a program needn't handle non-finite values.
Results may differ from a plain program's by a relative error of at most 0.001.
Values may be sent and summed in bfloat16 or wider, within the bound.
A program may use at most 64 MiB of HBM per device.

v0:
```python
import jax
import jax.numpy as jnp
from jax import lax
from jax.sharding import Mesh
from jax.sharding import PartitionSpec as P

SEQ = ("seq_0", "seq_1", "seq_2")
GRP_SEQ = ("grp", "seq_0", "seq_1", "seq_2")


def all_in_one(x, axis):
    leaves = jax.tree.leaves(x)
    turns = sorted(range(len(leaves)), key=lambda k: -leaves[k].size)
    width = (1, *leaves[turns[0]].shape)[-1]
    lines = [
        jnp.pad(leaves[k].reshape(-1), (0, -leaves[k].size % width)).reshape(-1, width)
        for k in turns
    ]
    both, at, found = (lax.all_gather(jnp.concatenate(lines), axis), 0, {})
    for k, line in zip(turns, lines):
        slab = both[:, at : at + len(line)].reshape(len(both), -1)
        found[k] = slab[:, : leaves[k].size].reshape(-1, *leaves[k].shape)
        at += len(line)
    numbers = iter(range(len(leaves)))
    return jax.tree.map(lambda _: found[next(numbers)], x)


def joined_all(x, axes, combine):
    for axis in axes:
        pieces = all_in_one(x, axis)
        x = jax.tree.map(lambda part: part[0], pieces)
        for k in range(1, lax.axis_size(axis)):
            x = combine(x, jax.tree.map(lambda part: part[k], pieces))
    return x


def combine(first, second):
    largest = jnp.maximum(first[0], second[0])
    factor_a = jnp.exp(first[0] - largest)
    factor_b = jnp.exp(second[0] - largest)
    totals = first[1] * factor_a + second[1] * factor_b
    accum = first[2] * factor_a[..., None] + second[2] * factor_b[..., None]
    return (largest, totals, accum)


def slot_info(global_ids, lengths, block_len, blk_seq, batch):
    seq_ids = global_ids // blk_seq
    starts = global_ids % blk_seq * block_len
    positions = starts[:, None] + jnp.arange(block_len, dtype=jnp.int32)[None, :]
    seq_hot = (seq_ids[:, None] == jnp.arange(batch, dtype=jnp.int32)[None, :]).astype(jnp.int32)
    slot_len = jnp.sum(seq_hot * lengths[None, :], axis=1)
    live = positions < slot_len[:, None]
    return (seq_hot, live)


def partials(cache, key_map, value_map, slot_query, live, seq_hot):
    rank = cache.shape[3] // 2
    head_dim = slot_query.shape[-1]
    scale = 1.0 / float(head_dim) ** 0.5
    highest = lax.Precision.HIGHEST
    key_lat = cache[..., :rank]
    value_lat = cache[..., rank:]
    keys = jnp.einsum("gstr,grkd->gstkd", key_lat, key_map, preferred_element_type=jnp.float32)
    scores = (
        jnp.einsum("gstkd,sgkjd->gskjt", keys, slot_query.astype(jnp.float32), precision=highest)
        * scale
    )
    live_wide = live[None, :, None, None, :]
    scores = jnp.where(live_wide, scores, -1e30)
    slot_max = jnp.max(scores, axis=-1)
    weights = jnp.where(live_wide, jnp.exp(scores - slot_max[..., None]), 0.0)
    slot_tot = jnp.sum(weights, axis=-1)
    values = jnp.einsum(
        "gstr,grkd->gstkd", value_lat, value_map, preferred_element_type=jnp.float32
    )
    slot_acc = jnp.einsum("gskjt,gstkd->gskjd", weights, values, precision=highest)
    hot_bool = seq_hot > 0
    hot_float = seq_hot.astype(jnp.float32)
    spread = jnp.where(hot_bool[None, :, None, None, :], slot_max[..., None], -1e30)
    seq_max = jnp.max(spread, axis=1)
    slot_seq_max = jnp.sum(
        jnp.where(hot_bool[None, :, None, None, :], seq_max[:, None], 0.0), axis=-1
    )
    factor = jnp.exp(slot_max - slot_seq_max)
    totals = jnp.einsum("gskj,sb->gkjb", slot_tot * factor, hot_float, precision=highest)
    accum = jnp.einsum(
        "gskjd,sb->gkjbd", slot_acc * factor[..., None], hot_float, precision=highest
    )
    return (seq_max, totals, accum)


def body(latent, up_key, up_value, queries, lengths, block_dest):
    groups = up_key.shape[0]
    dests = latent.shape[1]
    block_len = latent.shape[2]
    rank = latent.shape[3] // 2
    shards = block_dest.shape[0] // dests
    batch = queries.shape[0]
    q_heads = queries.shape[1]
    head_dim = queries.shape[2]
    per_group = up_key.shape[2] // head_dim
    per_kv = q_heads // (groups * per_group)
    blk_seq = block_dest.shape[0] // batch
    own_shard = lax.axis_index(SEQ)
    own_dests = lax.dynamic_slice_in_dim(block_dest, own_shard * dests, dests)
    source_order = (
        jnp.zeros((dests,), jnp.int32).at[own_dests].set(jnp.arange(dests, dtype=jnp.int32))
    )
    outgoing = latent[0][source_order]
    received = lax.all_to_all(outgoing, GRP_SEQ, split_axis=0, concat_axis=0, tiled=True)
    received = received.reshape(groups, shards, block_len, 2 * rank)
    decode_latent = received[None]
    key_map = up_key.reshape(groups, rank, per_group, head_dim)
    value_map = up_value.reshape(groups, rank, per_group, head_dim)
    query_rows = queries.reshape(batch, q_heads * head_dim)
    own_group = lax.axis_index("grp")
    slots = latent.shape[1]
    global_ids = own_shard * slots + jnp.arange(slots, dtype=jnp.int32)
    seq_hot, live = slot_info(global_ids, lengths, block_len, blk_seq, batch)
    picked = jnp.dot(seq_hot.astype(jnp.bfloat16), query_rows, preferred_element_type=jnp.float32)
    slot_query = picked.astype(jnp.bfloat16).reshape(slots, groups, per_group, per_kv, head_dim)
    group_query = lax.dynamic_slice_in_dim(slot_query, own_group, 1, 1)
    group_key = lax.dynamic_slice_in_dim(key_map, own_group, 1, 0)
    group_value = lax.dynamic_slice_in_dim(value_map, own_group, 1, 0)
    local = partials(latent, group_key, group_value, group_query, live, seq_hot)
    merged = joined_all(local, SEQ, combine)
    part_result = merged[2] / merged[1][..., None]
    result = lax.all_gather(part_result, "grp", axis=0, tiled=True)
    attended = jnp.transpose(result, (3, 0, 1, 2, 4)).reshape(batch, q_heads * head_dim)
    return (decode_latent, attended)


def solution(mesh):
    finer = Mesh(
        mesh.devices.reshape(mesh.shape["grp"], 4, 4, 2), ("grp", "seq_0", "seq_1", "seq_2")
    )
    in_specs = (P("grp", SEQ, None, None), P(), P(), P(), P(), P())
    out_specs = (P(GRP_SEQ, None, None, None, None), P())
    return jax.shard_map(body, mesh=finer, in_specs=in_specs, out_specs=out_specs, check_vma=False)
```

profile of v0, /device:TPU:0, one launch (start us, length us, event | category | flops | bytes accessed | tf_op | source)
XLA Modules:
  0.0 82.2 jit_solution(2277621008148799493)
XLA Ops:
  0.6 0.8 compare_select_fusion.1
  1.4 1.0 %scatter_custom_fusion = s32[128]{0:T(128)S(1)} fusion(s32[128]{0:T(128)S(1)} %compare_select_fusion.1, s32[128]{0:T(128)S(1)} %iota.27, s32[]{:T(128)} %constant.26.clone.1), kind=kCustom, calls=%fused_computation.172 | custom fusion | bytes 516 | tf_op jit(solution)/shard_map/scatter | solution.py:107
  2.4 3.6 %gather_fusion = bf16[128,32,256]{2,1,0:T(8,128)(2,1)} fusion(bf16[128,32,256]{2,1,0:T(8,128)(2,1)} %bitcast.358, s32[1024]{0:T(1024)S(1)} %pad_clamp_fusion), kind=kCustom, calls=%fused_computation | custom fusion | bytes 4194816 | tf_op jit(solution)/shard_map/gather | solution.py:109
  6.0 11.7 %all-to-all-start = ((bf16[128,32,256]{2,1,0:T(8,128)(2,1)}), bf16[128,32,256]{2,1,0:T(8,128)(2,1)}, u32[]{:S(2)}, u32[]{:S(2)}) async-start(bf16[128,32,256]{2,1,0:T(8,128)(2,1)} %gather_fusion), calls=%async_computation | async-start | bytes 4194304 | tf_op jit(solution)/shard_map/all_to_all | solution.py:110
  18.1 0.7 fusion.14
  18.8 0.2 copy-done.3
  19.0 0.7 fusion.4
  19.8 0.6 copy.35
  20.5 3.6 %fusion.102 = (f32[128,2,8]{2,1,0:T(2,128)S(1)}, f32[128,2,8,32]{3,2,1,0:T(8,128)S(1)}) fusion(f32[2,128,128,32]{1,3,0,2:T(8,128)S(1)} %fusion.14, bf16[128,4,2,8,128]{4,3,2,1,0:T(8,128)(2,1)S(1)} %bitcast.359, s32[]{:T(128)S(6)} %select_n.72, pred[128,32]{1,0:T(8,128)(4,1)S(1)} %add_compare_fusion), kind=kOutput, calls=%fused_computation.176 | convolution fusion | flops 100857856 | bytes 5005316 | tf_op jit(solution)/shard_map/gstkd,sgkjd->gskjt/dot_general | solution.py:65
  24.5 0.1 copy.26
  24.7 0.7 convolution_bitcast_fusion
  25.4 0.8 fusion.21
  26.2 3.7 %fusion.5 = f32[128,2,8,128]{3,2,1,0:T(8,128)S(1)} fusion(f32[128,32,2,128]{3,1,0,2:T(8,128)S(1)} %convolution_bitcast_fusion, f32[128,2,8,32]{3,2,1,0:T(8,128)S(1)} %get-tuple-element.30, f32[128,2,8]{2,1,0:T(2,128)S(1)} %copy.26, f32[128,2,8]{2,1,0:T(2,128)S(1)} %get-tuple-element.29, pred[128,32]{1,0:T(8,128)(4,1)S(1)} %add_compare_fusion), kind=kOutput, calls=%fused_computation.9 | convolution fusion | flops 101056512 | bytes 5525504 | tf_op jit(solution)/shard_map/gskjt,gstkd->gskjd/dot_general | solution.py:76
  29.9 0.9 %fusion.17 = f32[8,2,8,128]{3,0,2,1:T(8,128)S(1)} fusion(f32[128,2,8,128]{3,2,1,0:T(8,128)S(1)} %fusion.5, s32[128]{0:T(128)S(1)} %get-tuple-element.31), kind=kOutput, calls=%fused_computation.15 | convolution fusion | flops 25168896 | bytes 1114624 | tf_op jit(solution)/shard_map/gskjd,sb->gkjbd/dot_general | solution.py:86
  30.8 0.1 fusion.49
  31.1 18.3 %all-gather.3 = f32[4,130,128]{2,1,0:T(8,128)S(1)} all-gather(f32[1,130,128]{2,1,0:T(8,128)S(1)} %maximum_bitcast_fusion), channel_id=2, replica_groups=mesh['grp'=4,'seq_0'=4,'seq_1'=4,'seq_2'=2] {'seq_0'}, dimensions={0}, use_global_device_ids=true | all-gather | bytes 332800 | tf_op jit(solution)/shard_map/all_gather | solution.py:19
  49.4 0.2 fusion.39
  49.6 12.7 %all-gather.4 = f32[4,130,128]{2,1,0:T(8,128)S(1)} all-gather(f32[1,130,128]{2,1,0:T(8,128)S(1)} %maximum_bitcast_fusion.1), channel_id=3, replica_groups=mesh['grp'=4,'seq_0'=4,'seq_1'=4,'seq_2'=2] {'seq_1'}, dimensions={0}, use_global_device_ids=true | all-gather | bytes 332800 | tf_op jit(solution)/shard_map/all_gather | solution.py:19
  62.4 0.2 fusion.30
  62.6 1.9 %all-gather.5 = f32[2,130,128]{2,1,0:T(8,128)S(1)} all-gather(f32[1,130,128]{2,1,0:T(8,128)S(1)} %maximum_bitcast_fusion.2), channel_id=4, replica_groups=mesh['grp'=4,'seq_0'=4,'seq_1'=4,'seq_2'=2] {'seq_2'}, dimensions={0}, use_global_device_ids=true | all-gather | bytes 199680 | tf_op jit(solution)/shard_map/all_gather | solution.py:19
  64.9 0.1 add_divide_fusion
  65.0 13.4 %all_gather.27 = f32[4,2,8,8,128]{4,3,2,1,0:T(8,128)S(1)} all-gather(f32[1,2,8,8,128]{4,3,2,1,0:T(8,128)S(1)} %add_divide_fusion), channel_id=1, replica_groups=mesh['grp'=4,'seq_0'=4,'seq_1'=4,'seq_2'=2] {'grp'}, dimensions={0}, use_global_device_ids=true | all-gather | bytes 327680 | tf_op jit(solution)/shard_map/all_gather | solution.py:128
  78.4 3.1 %copy.52 = bf16[1,4,32,32,256]{4,3,2,1,0:T(8,128)(2,1)} copy(bf16[1,4,32,32,256]{4,3,2,1,0:T(8,128)(2,1)} %bitcast.1) | data formatting | bytes 4194304
  81.5 0.7 copy.53
  (43 shorter events, 1.5 us)
Async XLA Ops:
  6.0 11.8 %copy-start.4 = (s32[8]{0:T(128)S(1)}, s32[8]{0:T(128)}, u32[]{:S(2)}) copy-start(s32[8]{0:T(128)} %param.10) | copy-start | bytes 100
  6.0 11.9 %copy-start.1 = (bf16[4,128,256]{2,1,0:T(8,128)(2,1)S(1)}, bf16[4,128,256]{2,1,0:T(8,128)(2,1)}, u32[]{:S(2)}) copy-start(bf16[4,128,256]{2,1,0:T(8,128)(2,1)} %param.7) | copy-start | bytes 786436
  6.0 11.9 %copy-start.2 = (bf16[4,128,256]{2,1,0:T(8,128)(2,1)S(1)}, bf16[4,128,256]{2,1,0:T(8,128)(2,1)}, u32[]{:S(2)}) copy-start(bf16[4,128,256]{2,1,0:T(8,128)(2,1)} %param.8) | copy-start | bytes 786436
  6.0 12.1 %copy-start = (bf16[1,128,32,256]{3,2,1,0:T(8,128)(2,1)S(1)}, bf16[1,128,32,256]{3,2,1,0:T(8,128)(2,1)}, u32[]{:S(2)}) copy-start(bf16[1,128,32,256]{3,2,1,0:T(8,128)(2,1)} %param.6) | copy-start | bytes 6291460
  6.0 72.4 %all-to-all-start = ((bf16[128,32,256]{2,1,0:T(8,128)(2,1)}), bf16[128,32,256]{2,1,0:T(8,128)(2,1)}, u32[]{:S(2)}, u32[]{:S(2)}) async-start(bf16[128,32,256]{2,1,0:T(8,128)(2,1)} %gather_fusion), calls=%async_computation | async-start | bytes 4194304 | tf_op jit(solution)/shard_map/all_to_all | solution.py:110
  18.1 0.9 %copy-start.3 = (bf16[8,64,128]{2,1,0:T(8,128)(2,1)S(1)}, bf16[8,64,128]{2,1,0:T(8,128)(2,1)}, u32[]{:S(2)}) copy-start(bf16[8,64,128]{2,1,0:T(8,128)(2,1)} %param.9) | copy-start | bytes 393220
where the time goes:
time: 82.5 us; the launch traced here: 82.2 us
  blocking collectives  46.3 us (56%)
  starting transfers between devices  11.7 us (14%)
  matrix products  10.4 us (13%)
  local copies, waits for them, and re-layouts  10.2 us (12%)
  other arithmetic  2.58 us (3%)
  between operations  0.89 us (1%)
    all_gather x3, blocking collectives, all_in_one(): both, at, found = (lax.all_gather(jnp.concatenate(lines), axis), 0, {})  32.9 us
    all_gather x1, blocking collectives, body(): result = lax.all_gather(part_result, 'grp', axis=0, tiled=True)  13.4 us
    all_to_all x1, starting transfers between devices, body(): lax.all_to_all(outgoing, GRP_SEQ, split_axis=0, concat_axis=0, tiled=True)  11.7 us
    unnamed x13, local copies, waits for them, and re-layouts  4.61 us
    dot_general x1, matrix products, partials(): jnp.einsum('gskjt,gstkd->gskjd', weights, values, precision=highest)  3.68 us
    dot_general x1, matrix products, partials(): jnp.einsum('gstkd,sgkjd->gskjt', keys, slot_query.astype(jnp.float32), pr...  3.63 us
    gather x1, local copies, waits for them, and re-layouts, body(): outgoing = latent[0][source_order]  3.59 us
  transfers between devices with their start and end apart: 1, of which 0 were waited for; matrix products, arithmetic and copies ran while one was open for 17% of the time, Pallas kernels for 0%

commit v1 on v0

v1 whole, which is shorter than its diff:
```python
import functools
import random

import jax
import jax.numpy as jnp
from jax import lax
from jax.experimental import pallas as pl
from jax.experimental.pallas import tpu as pltpu
from jax.sharding import Mesh
from jax.sharding import PartitionSpec as P

AXES = ("grp", "seq_0", "seq_1", "seq_2")
SEQ = AXES[1:]
MESH = pl.DeviceIdType.MESH
F32 = jnp.float32
BF16 = jnp.bfloat16
LOG2E = 1.4426950408889634
NT = (((1,), (1,)), ((), ()))
NN = (((1,), (0,)), ((), ()))


def flow_order(sizes):
    nz, nx, ny, nc = sizes
    flows = [
        (dz, dx, dy, dc)
        for dz in range(nz)
        for dx in range(nx)
        for dy in range(ny)
        for dc in range(nc)
        if (dz, dx, dy, dc) != (0, 0, 0, 0)
    ]
    random.Random(1).shuffle(flows)
    return flows


def split3(x):
    hi = x.astype(BF16)
    rest = x - hi.astype(F32)
    mid = rest.astype(BF16)
    low = (rest - mid.astype(F32)).astype(BF16)
    return hi, mid, low


def split_dot(x, w, dims):
    n = x.shape[0]
    out = lax.dot_general(jnp.concatenate(split3(x), 0), w, dims, preferred_element_type=F32)
    return out[0:n] + out[n : 2 * n] + out[2 * n : 3 * n]


def exchange_kernel(
    sizes, first, second,
    latent, up_key, up_value, queries, lengths, block_dest,
    received, attended,
    lat, send, key_map, value_map, query, dest_row, order_v, order_s, length_s,
    scores, part_own, part_all, result, results,
    lat_sem, small_sem, order_sem, send_sem, recv_sem, part_send, part_recv,
    res_send, res_recv, relay_send, relay_recv,
):
    nz, nx, ny, nc = sizes
    z, x, y, c = [lax.axis_index(a) for a in AXES]
    shard = (x * ny + y) * nc + c
    me = z * (nx * ny * nc) + shard
    blocks, tokens = lat.shape[0], lat.shape[1]
    quads = shard % 4
    batch_id = shard // 4

    def peer(offset):
        dz, dx, dy, dc = offset
        return ((z + dz) % nz, (x + dx) % nx, (y + dy) % ny, (c + dc) % nc)

    def index_of(p):
        return ((p[0] * nx + p[1]) * ny + p[2]) * nc + p[3]

    flows = flow_order(sizes)
    barrier = pltpu.get_barrier_semaphore()
    for offset in flows:
        pl.semaphore_signal(barrier, 1, device_id=peer(offset), device_id_type=MESH)

    dest_copy = pltpu.make_async_copy(block_dest.at[pl.ds(shard, 1)], dest_row, small_sem.at[0])
    dest_copy.start()
    lat_copy = pltpu.make_async_copy(latent, lat, lat_sem)
    lat_copy.start()
    small = [
        pltpu.make_async_copy(up_key.at[z], key_map, small_sem.at[1]),
        pltpu.make_async_copy(up_value.at[z], value_map, small_sem.at[2]),
        pltpu.make_async_copy(queries.at[batch_id, pl.ds(pl.multiple_of(z * 16, 16), 16)], query, small_sem.at[3]),
        pltpu.make_async_copy(lengths, length_s, small_sem.at[4]),
    ]
    for copy in small:
        copy.start()

    dest_copy.wait()
    rows = lax.broadcasted_iota(jnp.int32, (blocks, blocks), 0)
    hot = jnp.where(rows == dest_row[...], 1.0, 0.0).astype(BF16)
    lanes = lax.broadcasted_iota(jnp.int32, (16, blocks), 1).astype(F32).astype(BF16)
    order = lax.dot_general(lanes, hot, NT, preferred_element_type=F32)[0:8].astype(jnp.int32)
    order_v[...] = jnp.clip(order, 0, blocks - 1)
    order_copy = pltpu.make_async_copy(order_v.at[pl.ds(0, 1)], order_s, order_sem)
    order_copy.start()
    order_copy.wait()
    lat_copy.wait()

    @pl.loop(0, blocks, unroll=8)
    def _(d):
        send[d] = lat[order_s[0, d]]

    received[me] = send[me]

    pl.semaphore_wait(barrier, len(flows))

    def send_blocks(some):
        for offset in some:
            p = peer(offset)
            pltpu.make_async_remote_copy(
                send.at[index_of(p)], received.at[me], send_sem, recv_sem, device_id=p, device_id_type=MESH
            ).start()

    send_blocks(flows[:first])

    for copy in small:
        copy.wait()
    head_dim = query.shape[1]
    rank = lat.shape[2] // 2
    q0 = lax.dot_general(query[...], key_map[:, 0:head_dim], NT, preferred_element_type=F32)
    q1 = lax.dot_general(query[...], key_map[:, head_dim : 2 * head_dim], NT, preferred_element_type=F32)
    scale = LOG2E / float(head_dim) ** 0.5
    q_parts = jnp.concatenate(split3(jnp.concatenate([q0[0:8], q1[8:16]], 0) * scale), 0)
    length = length_s[batch_id]
    start = quads * (blocks * tokens)
    chunk_blocks = 16
    width = chunk_blocks * tokens
    best = jnp.full((16, 128), -1e30, F32)
    for i in range(blocks // chunk_blocks):
        keys = lat[i * chunk_blocks : (i + 1) * chunk_blocks, :, 0:rank].reshape(width, rank)
        s3 = lax.dot_general(q_parts, keys, NT, preferred_element_type=F32)
        s = s3[0:16] + s3[16:32] + s3[32:48]
        position = start + i * width + lax.broadcasted_iota(jnp.int32, (16, width), 1)
        s = jnp.where(position < length, s, -1e30)
        scores[:, i * width : (i + 1) * width] = s
        for j in range(width // 128):
            best = jnp.maximum(best, s[:, j * 128 : (j + 1) * 128])
    top = jnp.max(best, axis=1, keepdims=True)
    total = jnp.zeros((16, 128), F32)
    acc = jnp.zeros((32, rank), F32)
    for i in range(blocks // chunk_blocks):
        s = scores[:, i * width : (i + 1) * width]
        position = start + i * width + lax.broadcasted_iota(jnp.int32, (16, width), 1)
        w = jnp.where(position < length, jnp.exp2(s - top), 0.0)
        for j in range(width // 128):
            total = total + w[:, j * 128 : (j + 1) * 128]
        hi = w.astype(BF16)
        low = (w - hi.astype(F32)).astype(BF16)
        vals = lat[i * chunk_blocks : (i + 1) * chunk_blocks, :, rank : 2 * rank].reshape(width, rank)
        acc = acc + lax.dot_general(jnp.concatenate([hi, low], 0), vals, NN, preferred_element_type=F32)
    part_own[0:16] = acc[0:16] + acc[16:32]
    part_own[16:32] = jnp.broadcast_to(top, (16, 128))
    part_own[32:48] = jnp.broadcast_to(jnp.sum(total, axis=1, keepdims=True), (16, 128))
    part_all[quads] = part_own[...]

    for k in range(1, 4):
        other_y = y + (k // 2) * (1 - 2 * (y % 2))
        other_c = (c + k % 2) % 2
        pltpu.make_async_remote_copy(
            part_own, part_all.at[quads], part_send, part_recv, device_id=(z, x, other_y, other_c), device_id_type=MESH
        ).start()

    send_blocks(flows[first:second])

    three = part_all.at[pl.ds(0, 3)]
    pltpu.make_async_copy(three, three, part_recv).wait()
    tops = [part_all[k, 16:32] for k in range(4)]
    top = jnp.maximum(jnp.maximum(tops[0], tops[1]), jnp.maximum(tops[2], tops[3]))
    total = jnp.zeros((16, 128), F32)
    acc = jnp.zeros((16, 128), F32)
    for k in range(4):
        factor = jnp.exp2(tops[k] - top)
        total = total + part_all[k, 32:48] * factor
        acc = acc + part_all[k, 0:16] * factor
    mean = acc / total
    r0 = split_dot(mean[0:8], value_map[:, 0:head_dim], NN)
    r1 = split_dot(mean[8:16], value_map[:, head_dim : 2 * head_dim], NN)
    result[0:8] = r0
    result[8:16] = r1

    half = y // 2
    slot = half * (nx * nz) + x * nz + z
    dest_y = (y + c * (2 * (y % 2) - 1) + ny) % ny
    for dx, dz in random.Random(2).sample([(i, j) for i in range(nx) for j in range(nz)], nx * nz):
        pltpu.make_async_remote_copy(
            result, results.at[slot], res_send, res_recv,
            device_id=((z + dz) % nz, (x + dx) % nx, dest_y, 1 - c), device_id_type=MESH,
        ).start()

    send_blocks(flows[second:])

    per_half = nx * nz
    mine = c * half + (1 - c) * (1 - half)
    got = results.at[pl.ds(mine * per_half, per_half)]
    pltpu.make_async_copy(got, got, res_recv).wait()
    relay = pltpu.make_async_remote_copy(
        got, got, relay_send, relay_recv, device_id=(z, x, y, 1 - c), device_id_type=MESH
    )
    relay.start()
    relay.wait()
    for j in range(2):
        for zz in range(nz):
            for h in range(16):
                for xx in range(nx):
                    col = (zz * 16 + h) * 128
                    row = 2 * xx + j
                    attended[row : row + 1, col : col + 128] = results[j * per_half + xx * nz + zz, h : h + 1]

    pltpu.make_async_copy(part_all.at[pl.ds(0, 3)], part_all.at[pl.ds(0, 3)], part_send).wait()
    sixteen = results.at[pl.ds(0, per_half)]
    pltpu.make_async_copy(sixteen, sixteen, res_send).wait()
    rest = received.at[pl.ds(0, len(flows))]
    pltpu.make_async_copy(rest, rest, send_sem).wait()
    pltpu.make_async_copy(rest, rest, recv_sem).wait()


def store_kernel(received, attended, out0, out1, sem):
    a = pltpu.make_async_copy(received, out0, sem.at[0])
    b = pltpu.make_async_copy(attended, out1, sem.at[1])
    a.start()
    b.start()
    a.wait()
    b.wait()


def body(latent, up_key, up_value, queries, lengths, block_dest):
    sizes = tuple(lax.axis_size(a) for a in AXES)
    groups, rank, width = up_key.shape
    blocks, tokens, both = latent.shape[1:]
    batch, heads, head_dim = queries.shape
    hbm = pl.BlockSpec(memory_space=pltpu.MemorySpace.HBM)
    vmem = pl.BlockSpec(memory_space=pltpu.MemorySpace.VMEM)
    dma = pltpu.SemaphoreType.DMA
    received, attended = pl.pallas_call(
        functools.partial(exchange_kernel, sizes, 50, 90),
        out_shape=(pltpu.VMEM((blocks, tokens, both), BF16), pltpu.VMEM((batch, heads * head_dim), F32)),
        in_specs=[hbm] * 6,
        out_specs=(vmem, vmem),
        scratch_shapes=[
            pltpu.VMEM((blocks, tokens, both), BF16),
            pltpu.VMEM((blocks, tokens, both), BF16),
            pltpu.VMEM((rank, width), BF16),
            pltpu.VMEM((rank, width), BF16),
            pltpu.VMEM((heads // groups, head_dim), BF16),
            pltpu.VMEM((1, blocks), jnp.int32),
            pltpu.VMEM((8, blocks), jnp.int32),
            pltpu.SMEM((1, blocks), jnp.int32),
            pltpu.SMEM((batch,), jnp.int32),
            pltpu.VMEM((16, blocks * tokens), F32),
            pltpu.VMEM((48, 128), F32),
            pltpu.VMEM((4, 48, 128), F32),
            pltpu.VMEM((16, 128), F32),
            pltpu.VMEM((groups * batch, 16, 128), F32),
            dma, dma((5,)), dma, dma, dma, dma, dma, dma, dma, dma, dma,
        ],
        compiler_params=pltpu.CompilerParams(collective_id=1, has_side_effects=True),
        name="exchange",
    )(latent[0], up_key, up_value, queries, lengths, block_dest.reshape(-1, blocks))
    decode_latent, attended = pl.pallas_call(
        store_kernel,
        out_shape=(
            jax.ShapeDtypeStruct((blocks, tokens, both), BF16),
            jax.ShapeDtypeStruct((batch, heads * head_dim), F32),
        ),
        in_specs=[vmem, vmem],
        out_specs=(hbm, hbm),
        scratch_shapes=[dma((2,))],
        name="store",
    )(*[pltpu.with_memory_space_constraint(a, pltpu.MemorySpace.VMEM) for a in (received, attended)])
    return decode_latent.reshape(1, groups, blocks // groups, tokens, both), attended


def solution(mesh):
    finer = Mesh(mesh.devices.reshape(mesh.shape["grp"], 4, 4, 2), AXES)
    in_specs = (P("grp", SEQ, None, None), P(), P(), P(), P(), P())
    out_specs = (P(AXES, None, None, None, None), P())
    return jax.shard_map(body, mesh=finer, in_specs=in_specs, out_specs=out_specs, check_vma=False)
```

time: 82.5 us -> 41.9 us (0.51)
  blocking collectives: 46.3 us -> 0 us
  Pallas kernels: 0 us -> 40.5 us
  starting transfers between devices: 11.7 us -> 0 us
  matrix products: 10.4 us -> 0 us
  local copies, waits for them, and re-layouts: 10.2 us -> 0 us
  other arithmetic: 2.58 us -> 0 us
    all_gather x4 -> x0, blocking collectives: 46.3 us -> none  [the longest x3 32.9 us: all_in_one(): both, at, found = (lax.all_gather(jnp.concatenate(lines), axis), 0, {})]
    pallas_call x0 -> x2, Pallas kernels: none -> 40.5 us  [the longest x1 39.1 us: body(): pl.pallas_call(functools.partial(exchange_kernel, sizes, 50, 90), out_sha...]
    all_to_all x1 -> x0, starting transfers between devices: 11.7 us -> none  [body(): lax.all_to_all(outgoing, GRP_SEQ, split_axis=0, concat_axis=0, tiled=True)]
    dot_general x7 -> x0, matrix products: 10.4 us -> none  [the longest x1 3.68 us: partials(): jnp.einsum('gskjt,gstkd->gskjd', weights, values, precision=highest)]
    unnamed x13 -> x0, local copies, waits for them, and re-layouts: 4.61 us -> none
    gather x1 -> x0, local copies, waits for them, and re-layouts: 3.59 us -> none  [body(): outgoing = latent[0][source_order]]
    scatter x1 -> x0, local copies, waits for them, and re-layouts: 0.97 us -> none  [body(): jnp.zeros((dests,), jnp.int32).at[own_dests]]
    reduce_sum x3 -> x0, other arithmetic: 0.97 us -> none  [the longest x1 0.8 us: partials(): slot_tot = jnp.sum(weights, axis=-1)]
  transfers between devices with their start and end apart: 1 -> 0, of which waited for: 0 -> 0; matrix products, arithmetic and copies ran while one was open for 17% -> 0% of each run, Pallas kernels for 0% -> 0%
where the time goes in v1:
time: 41.9 us; the launch traced here: 41.2 us
  Pallas kernels  40.5 us (97%)
  between operations  0.64 us (2%)
    pallas_call x1, Pallas kernels, body(): pl.pallas_call(functools.partial(exchange_kernel, sizes, 50, 90), out_sha...  39.1 us
    pallas_call x1, Pallas kernels, body(): pl.pallas_call(store_kernel, out_shape=(jax.ShapeDtypeStruct((blocks, tok...  1.41 us

profile of v1, /device:TPU:0, one launch (start us, length us, event | category | flops | bytes accessed | tf_op | source)
XLA Modules:
  0.0 41.2 jit_solution(1329358309345539672)
XLA Ops:
  0.6 39.1 %exchange.1 = (bf16[128,32,256]{2,1,0:T(8,128)(2,1)S(1)}, f32[8,8192]{1,0:T(8,128)S(1)}) custom-call(bf16[128,32,256]{2,1,0:T(8,128)(2,1)} %bitcast.3, bf16[4,128,256]{2,1,0:T(8,128)(2,1)} %up_key.1, bf16[4,128,256]{2,1,0:T(8,128)(2,1)} %up_value.1, bf16[8,64,128]{2,1,0:T(8,128)(2,1)} %queries.1, s32[8]{0:T(128)} %lengths.1, s32[32,128]{1,0:T(8,128)} %bitcast.4), custom_call_target="tpu_custom_call" | custom-call | tf_op jit(solution)/shard_map/exchange/pallas_call | solution.py:238
  39.7 1.4 %store.1 = (bf16[128,32,256]{2,1,0:T(8,128)(2,1)}, f32[8,8192]{1,0:T(8,128)}) custom-call(bf16[128,32,256]{2,1,0:T(8,128)(2,1)S(1)} %get-tuple-element.6.received, f32[8,8192]{1,0:T(8,128)S(1)} %get-tuple-element.7.attended), custom_call_target="tpu_custom_call" | custom-call | tf_op jit(solution)/shard_map/store/pallas_call | solution.py:263

commit v2 on v1

--- a/solution.py
+++ b/solution.py
@@ -17,20 +17,21 @@
 LOG2E = 1.4426950408889634
 NT = (((1,), (1,)), ((), ()))
 NN = (((1,), (0,)), ((), ()))
-
-
-def flow_order(sizes):
+SEED = 1
+
+
+def flow_stages(sizes):
     nz, nx, ny, nc = sizes
-    flows = [
-        (dz, dx, dy, dc)
-        for dz in range(nz)
-        for dx in range(nx)
-        for dy in range(ny)
-        for dc in range(nc)
-        if (dz, dx, dy, dc) != (0, 0, 0, 0)
-    ]
-    random.Random(1).shuffle(flows)
-    return flows
+    stages = [[], [], [], []]
+    for dz in range(nz):
+        for dx in range(nx):
+            for dy in range(ny):
+                for dc in range(nc):
+                    stages[(dz > 0) + (dx > 0) + (dy > 0)].append((dz, dx, dy, dc))
+    near = stages[0][1:] + stages[1]
+    for k, stage in enumerate((near, stages[2], stages[3])):
+        random.Random(SEED + k).shuffle(stage)
+    return near, stages[2], stages[3]
 
 
 def split3(x):
@@ -48,13 +49,13 @@
 
 
 def exchange_kernel(
-    sizes, first, second,
+    sizes, first,
     latent, up_key, up_value, queries, lengths, block_dest,
     received, attended,
     lat, send, key_map, value_map, query, dest_row, order_v, order_s, length_s,
     scores, part_own, part_all, result, results,
     lat_sem, small_sem, order_sem, send_sem, recv_sem, part_send, part_recv,
-    res_send, res_recv, relay_send, relay_recv,
+    res_send, res_recv, relay_send, relay_recv, in_x, in_y, in_all,
 ):
     nz, nx, ny, nc = sizes
     z, x, y, c = [lax.axis_index(a) for a in AXES]
@@ -71,10 +72,15 @@
     def index_of(p):
         return ((p[0] * nx + p[1]) * ny + p[2]) * nc + p[3]
 
-    flows = flow_order(sizes)
+    near, planes, cube = flow_stages(sizes)
+    rings = [[(dz, 0, 0, 0) for dz in range(1, nz)], [(0, dx, 0, 0) for dx in range(1, nx)], [(0, 0, dy, 0) for dy in range(1, ny)]]
     barrier = pltpu.get_barrier_semaphore()
-    for offset in flows:
-        pl.semaphore_signal(barrier, 1, device_id=peer(offset), device_id_type=MESH)
+
+    def tell(semaphore, offsets):
+        for offset in offsets:
+            pl.semaphore_signal(semaphore, 1, device_id=peer(offset), device_id_type=MESH)
+
+    tell(barrier, near)
 
     dest_copy = pltpu.make_async_copy(block_dest.at[pl.ds(shard, 1)], dest_row, small_sem.at[0])
     dest_copy.start()
@@ -106,8 +112,6 @@
 
     received[me] = send[me]
 
-    pl.semaphore_wait(barrier, len(flows))
-
     def send_blocks(some):
         for offset in some:
             p = peer(offset)
@@ -115,7 +119,10 @@
                 send.at[index_of(p)], received.at[me], send_sem, recv_sem, device_id=p, device_id_type=MESH
             ).start()
 
-    send_blocks(flows[:first])
+    pl.semaphore_wait(barrier, len(near))
+    tell(in_x, rings[1])
+    tell(in_y, rings[2])
+    send_blocks(near)
 
     for copy in small:
         copy.wait()
@@ -164,7 +171,10 @@
             part_own, part_all.at[quads], part_send, part_recv, device_id=(z, x, other_y, other_c), device_id_type=MESH
         ).start()
 
-    send_blocks(flows[first:second])
+    pl.semaphore_wait(in_x, nx - 1)
+    pl.semaphore_wait(in_y, ny - 1)
+    tell(in_all, rings[1])
+    send_blocks(planes)
 
     three = part_all.at[pl.ds(0, 3)]
     pltpu.make_async_copy(three, three, part_recv).wait()
@@ -182,6 +192,9 @@
     result[0:8] = r0
     result[8:16] = r1
 
+    pl.semaphore_wait(in_all, nx - 1)
+    send_blocks(cube[:first])
+
     half = y // 2
     slot = half * (nx * nz) + x * nz + z
     dest_y = (y + c * (2 * (y % 2) - 1) + ny) % ny
@@ -191,7 +204,7 @@
             device_id=((z + dz) % nz, (x + dx) % nx, dest_y, 1 - c), device_id_type=MESH,
         ).start()
 
-    send_blocks(flows[second:])
+    send_blocks(cube[first:])
 
     per_half = nx * nz
     mine = c * half + (1 - c) * (1 - half)
@@ -213,7 +226,7 @@
     pltpu.make_async_copy(part_all.at[pl.ds(0, 3)], part_all.at[pl.ds(0, 3)], part_send).wait()
     sixteen = results.at[pl.ds(0, per_half)]
     pltpu.make_async_copy(sixteen, sixteen, res_send).wait()
-    rest = received.at[pl.ds(0, len(flows))]
+    rest = received.at[pl.ds(0, blocks - 1)]
     pltpu.make_async_copy(rest, rest, send_sem).wait()
     pltpu.make_async_copy(rest, rest, recv_sem).wait()
 
@@ -236,7 +249,7 @@
     vmem = pl.BlockSpec(memory_space=pltpu.MemorySpace.VMEM)
     dma = pltpu.SemaphoreType.DMA
     received, attended = pl.pallas_call(
-        functools.partial(exchange_kernel, sizes, 50, 90),
+        functools.partial(exchange_kernel, sizes, 12),
         out_shape=(pltpu.VMEM((blocks, tokens, both), BF16), pltpu.VMEM((batch, heads * head_dim), F32)),
         in_specs=[hbm] * 6,
         out_specs=(vmem, vmem),
@@ -256,6 +269,7 @@
             pltpu.VMEM((16, 128), F32),
             pltpu.VMEM((groups * batch, 16, 128), F32),
             dma, dma((5,)), dma, dma, dma, dma, dma, dma, dma, dma, dma,
+            pltpu.SemaphoreType.REGULAR, pltpu.SemaphoreType.REGULAR, pltpu.SemaphoreType.REGULAR,
         ],
         compiler_params=pltpu.CompilerParams(collective_id=1, has_side_effects=True),
         name="exchange",

time: 41.9 us -> 38.8 us (0.926)
  Pallas kernels: 40.5 us -> 37.8 us
    pallas_call x1, Pallas kernels: 39.1 us -> 36.4 us  [body(): pl.pallas_call(functools.partial(exchange_kernel, sizes, 12), out_shape=(...]
where the time goes in v2:
time: 38.8 us; the launch traced here: 38.4 us
  Pallas kernels  37.8 us (97%)
  between operations  0.64 us (2%)
    pallas_call x1, Pallas kernels, body(): pl.pallas_call(functools.partial(exchange_kernel, sizes, 12), out_shape=(...  36.4 us
    pallas_call x1, Pallas kernels, body(): pl.pallas_call(store_kernel, out_shape=(jax.ShapeDtypeStruct((blocks, tok...  1.41 us

profile of v2, /device:TPU:0, one launch (start us, length us, event | category | flops | bytes accessed | tf_op | source)
XLA Modules:
  0.0 38.4 jit_solution(212503450455010865)
XLA Ops:
  0.6 36.4 %exchange.1 = (bf16[128,32,256]{2,1,0:T(8,128)(2,1)S(1)}, f32[8,8192]{1,0:T(8,128)S(1)}) custom-call(bf16[128,32,256]{2,1,0:T(8,128)(2,1)} %bitcast.3, bf16[4,128,256]{2,1,0:T(8,128)(2,1)} %up_key.1, bf16[4,128,256]{2,1,0:T(8,128)(2,1)} %up_value.1, bf16[8,64,128]{2,1,0:T(8,128)(2,1)} %queries.1, s32[8]{0:T(128)} %lengths.1, s32[32,128]{1,0:T(8,128)} %bitcast.4), custom_call_target="tpu_custom_call" | custom-call | tf_op jit(solution)/shard_map/exchange/pallas_call | solution.py:251
  37.0 1.4 %store.1 = (bf16[128,32,256]{2,1,0:T(8,128)(2,1)}, f32[8,8192]{1,0:T(8,128)}) custom-call(bf16[128,32,256]{2,1,0:T(8,128)(2,1)S(1)} %get-tuple-element.6.received, f32[8,8192]{1,0:T(8,128)S(1)} %get-tuple-element.7.attended), custom_call_target="tpu_custom_call" | custom-call | tf_op jit(solution)/shard_map/store/pallas_call | solution.py:277

commit v3 on v2

--- a/solution.py
+++ b/solution.py
@@ -17,7 +17,32 @@
 LOG2E = 1.4426950408889634
 NT = (((1,), (1,)), ((), ()))
 NN = (((1,), (0,)), ((), ()))
-SEED = 1
+SEED = 7
+EARLY = 36
+
+
+def loads_of(flow):
+    loads = []
+    for steps in flow[:3]:
+        loads += {0: [0, 0], 1: [1, 0], 2: [1, 1], 3: [0, 1]}[steps]
+    return loads
+
+
+def balanced(flows, total, seed):
+    left = list(flows)
+    random.Random(seed).shuffle(left)
+    order = []
+    while left:
+        def uneven(flow):
+            after = [a + b for a, b in zip(total, loads_of(flow))]
+            mean = sum(after) / len(after)
+            return sum((a - mean) ** 2 for a in after)
+
+        best = min(left, key=uneven)
+        left.remove(best)
+        order.append(best)
+        total[:] = [a + b for a, b in zip(total, loads_of(best))]
+    return order
 
 
 def flow_stages(sizes):
@@ -28,10 +53,11 @@
             for dy in range(ny):
                 for dc in range(nc):
                     stages[(dz > 0) + (dx > 0) + (dy > 0)].append((dz, dx, dy, dc))
-    near = stages[0][1:] + stages[1]
-    for k, stage in enumerate((near, stages[2], stages[3])):
-        random.Random(SEED + k).shuffle(stage)
-    return near, stages[2], stages[3]
+    total = [0] * 6
+    near = balanced(stages[0][1:] + stages[1], total, SEED)
+    second = balanced(stages[2], total, SEED + 1)
+    third = balanced(second[EARLY:] + stages[3], total, SEED + 2)
+    return near, second[:EARLY], third
 
 
 def split3(x):
@@ -49,7 +75,7 @@
 
 
 def exchange_kernel(
-    sizes, first,
+    sizes,
     latent, up_key, up_value, queries, lengths, block_dest,
     received, attended,
     lat, send, key_map, value_map, query, dest_row, order_v, order_s, length_s,
@@ -80,12 +106,14 @@
         for offset in offsets:
             pl.semaphore_signal(semaphore, 1, device_id=peer(offset), device_id_type=MESH)
 
-    tell(barrier, near)
 
     dest_copy = pltpu.make_async_copy(block_dest.at[pl.ds(shard, 1)], dest_row, small_sem.at[0])
     dest_copy.start()
     lat_copy = pltpu.make_async_copy(latent, lat, lat_sem)
-    lat_copy.start()
+    piece = blocks // 8
+    for k in range(8):
+        part = pl.ds(k * piece, piece)
+        pltpu.make_async_copy(latent.at[part], lat.at[part], lat_sem).start()
     small = [
         pltpu.make_async_copy(up_key.at[z], key_map, small_sem.at[1]),
         pltpu.make_async_copy(up_value.at[z], value_map, small_sem.at[2]),
@@ -95,6 +123,8 @@
     for copy in small:
         copy.start()
 
+    tell(barrier, near)
+
     dest_copy.wait()
     rows = lax.broadcasted_iota(jnp.int32, (blocks, blocks), 0)
     hot = jnp.where(rows == dest_row[...], 1.0, 0.0).astype(BF16)
@@ -103,6 +133,11 @@
     order_v[...] = jnp.clip(order, 0, blocks - 1)
     order_copy = pltpu.make_async_copy(order_v.at[pl.ds(0, 1)], order_s, order_sem)
     order_copy.start()
+
+    pl.semaphore_wait(barrier, len(near))
+    tell(in_x, rings[1])
+    tell(in_y, rings[2])
+
     order_copy.wait()
     lat_copy.wait()
 
@@ -119,9 +154,6 @@
                 send.at[index_of(p)], received.at[me], send_sem, recv_sem, device_id=p, device_id_type=MESH
             ).start()
 
-    pl.semaphore_wait(barrier, len(near))
-    tell(in_x, rings[1])
-    tell(in_y, rings[2])
     send_blocks(near)
 
     for copy in small:
@@ -176,6 +208,8 @@
     tell(in_all, rings[1])
     send_blocks(planes)
 
+    pl.semaphore_wait(in_all, nx - 1)
+
     three = part_all.at[pl.ds(0, 3)]
     pltpu.make_async_copy(three, three, part_recv).wait()
     tops = [part_all[k, 16:32] for k in range(4)]
@@ -192,9 +226,6 @@
     result[0:8] = r0
     result[8:16] = r1
 
-    pl.semaphore_wait(in_all, nx - 1)
-    send_blocks(cube[:first])
-
     half = y // 2
     slot = half * (nx * nz) + x * nz + z
     dest_y = (y + c * (2 * (y % 2) - 1) + ny) % ny
@@ -204,7 +235,7 @@
             device_id=((z + dz) % nz, (x + dx) % nx, dest_y, 1 - c), device_id_type=MESH,
         ).start()
 
-    send_blocks(cube[first:])
+    send_blocks(cube)
 
     per_half = nx * nz
     mine = c * half + (1 - c) * (1 - half)
@@ -232,12 +263,14 @@
 
 
 def store_kernel(received, attended, out0, out1, sem):
-    a = pltpu.make_async_copy(received, out0, sem.at[0])
-    b = pltpu.make_async_copy(attended, out1, sem.at[1])
-    a.start()
-    b.start()
-    a.wait()
-    b.wait()
+    copies = [
+        pltpu.make_async_copy(received, out0, sem.at[0]),
+        pltpu.make_async_copy(attended, out1, sem.at[1]),
+    ]
+    for copy in copies:
+        copy.start()
+    for copy in copies:
+        copy.wait()
 
 
 def body(latent, up_key, up_value, queries, lengths, block_dest):
@@ -249,7 +282,7 @@
     vmem = pl.BlockSpec(memory_space=pltpu.MemorySpace.VMEM)
     dma = pltpu.SemaphoreType.DMA
     received, attended = pl.pallas_call(
-        functools.partial(exchange_kernel, sizes, 12),
+        functools.partial(exchange_kernel, sizes),
         out_shape=(pltpu.VMEM((blocks, tokens, both), BF16), pltpu.VMEM((batch, heads * head_dim), F32)),
         in_specs=[hbm] * 6,
         out_specs=(vmem, vmem),

time: 38.8 us -> 38.3 us (0.987)
  Pallas kernels: 37.8 us -> 37.2 us
    pallas_call x1, Pallas kernels: 36.4 us -> 35.7 us  [body(): pl.pallas_call(functools.partial(exchange_kernel, sizes), out_shape=(pltp...]
where the time goes in v3:
time: 38.3 us; the launch traced here: 37.8 us
  Pallas kernels  37.2 us (97%)
  between operations  0.64 us (2%)
    pallas_call x1, Pallas kernels, body(): pl.pallas_call(functools.partial(exchange_kernel, sizes), out_shape=(pltp...  35.7 us
    pallas_call x1, Pallas kernels, body(): pl.pallas_call(store_kernel, out_shape=(jax.ShapeDtypeStruct((blocks, tok...  1.41 us

profile of v3, /device:TPU:0, one launch (start us, length us, event | category | flops | bytes accessed | tf_op | source)
XLA Modules:
  0.0 37.8 jit_solution(8325557939305833237)
XLA Ops:
  0.6 35.7 %exchange.1 = (bf16[128,32,256]{2,1,0:T(8,128)(2,1)S(1)}, f32[8,8192]{1,0:T(8,128)S(1)}) custom-call(bf16[128,32,256]{2,1,0:T(8,128)(2,1)} %bitcast.3, bf16[4,128,256]{2,1,0:T(8,128)(2,1)} %up_key.1, bf16[4,128,256]{2,1,0:T(8,128)(2,1)} %up_value.1, bf16[8,64,128]{2,1,0:T(8,128)(2,1)} %queries.1, s32[8]{0:T(128)} %lengths.1, s32[32,128]{1,0:T(8,128)} %bitcast.4), custom_call_target="tpu_custom_call" | custom-call | tf_op jit(solution)/shard_map/exchange/pallas_call | solution.py:284
  36.4 1.4 %store.1 = (bf16[128,32,256]{2,1,0:T(8,128)(2,1)}, f32[8,8192]{1,0:T(8,128)}) custom-call(bf16[128,32,256]{2,1,0:T(8,128)(2,1)S(1)} %get-tuple-element.6.received, f32[8,8192]{1,0:T(8,128)S(1)} %get-tuple-element.7.attended), custom_call_target="tpu_custom_call" | custom-call | tf_op jit(solution)/shard_map/store/pallas_call | solution.py:310

commit v4 on v3

--- a/solution.py
+++ b/solution.py
@@ -17,7 +17,7 @@
 LOG2E = 1.4426950408889634
 NT = (((1,), (1,)), ((), ()))
 NN = (((1,), (0,)), ((), ()))
-SEED = 7
+SEED = 3
 EARLY = 36
 
 
@@ -134,26 +134,27 @@
     order_copy = pltpu.make_async_copy(order_v.at[pl.ds(0, 1)], order_s, order_sem)
     order_copy.start()
 
+    order_copy.wait()
+    lat_copy.wait()
+
+    @pl.loop(0, blocks, unroll=8)
+    def _(d):
+        send[d] = lat[order_s[0, d]]
+
+    received[me] = send[me]
+
+    turn = 1 - 2 * c
+
+    def send_blocks(some):
+        for dz, dx, dy, dc in some:
+            p = peer((turn * dz + nz, turn * dx + nx, turn * dy + ny, dc))
+            pltpu.make_async_remote_copy(
+                send.at[index_of(p)], received.at[me], send_sem, recv_sem, device_id=p, device_id_type=MESH
+            ).start()
+
     pl.semaphore_wait(barrier, len(near))
     tell(in_x, rings[1])
     tell(in_y, rings[2])
-
-    order_copy.wait()
-    lat_copy.wait()
-
-    @pl.loop(0, blocks, unroll=8)
-    def _(d):
-        send[d] = lat[order_s[0, d]]
-
-    received[me] = send[me]
-
-    def send_blocks(some):
-        for offset in some:
-            p = peer(offset)
-            pltpu.make_async_remote_copy(
-                send.at[index_of(p)], received.at[me], send_sem, recv_sem, device_id=p, device_id_type=MESH
-            ).start()
-
     send_blocks(near)
 
     for copy in small:
@@ -196,6 +197,10 @@
     part_own[32:48] = jnp.broadcast_to(jnp.sum(total, axis=1, keepdims=True), (16, 128))
     part_all[quads] = part_own[...]
 
+    pl.semaphore_wait(in_x, nx - 1)
+    pl.semaphore_wait(in_y, ny - 1)
+    tell(in_all, rings[1])
+
     for k in range(1, 4):
         other_y = y + (k // 2) * (1 - 2 * (y % 2))
         other_c = (c + k % 2) % 2
@@ -203,9 +208,6 @@
             part_own, part_all.at[quads], part_send, part_recv, device_id=(z, x, other_y, other_c), device_id_type=MESH
         ).start()
 
-    pl.semaphore_wait(in_x, nx - 1)
-    pl.semaphore_wait(in_y, ny - 1)
-    tell(in_all, rings[1])
     send_blocks(planes)
 
     pl.semaphore_wait(in_all, nx - 1)
@@ -226,6 +228,8 @@
     result[0:8] = r0
     result[8:16] = r1
 
+    send_blocks(cube[:6])
+
     half = y // 2
     slot = half * (nx * nz) + x * nz + z
     dest_y = (y + c * (2 * (y % 2) - 1) + ny) % ny
@@ -235,7 +239,7 @@
             device_id=((z + dz) % nz, (x + dx) % nx, dest_y, 1 - c), device_id_type=MESH,
         ).start()
 
-    send_blocks(cube)
+    send_blocks(cube[6:])
 
     per_half = nx * nz
     mine = c * half + (1 - c) * (1 - half)

time: 38.3 us -> 38 us (level)
  Pallas kernels: 37.2 us -> 36.7 us
    pallas_call x1, Pallas kernels: 35.7 us -> 35.3 us  [body(): pl.pallas_call(functools.partial(exchange_kernel, sizes), out_shape=(pltp...]
where the time goes in v4:
time: 38 us; the launch traced here: 37.4 us
  Pallas kernels  36.7 us (97%)
  between operations  0.64 us (2%)
    pallas_call x1, Pallas kernels, body(): pl.pallas_call(functools.partial(exchange_kernel, sizes), out_shape=(pltp...  35.3 us
    pallas_call x1, Pallas kernels, body(): pl.pallas_call(store_kernel, out_shape=(jax.ShapeDtypeStruct((blocks, tok...  1.41 us

profile of v4, /device:TPU:0, one launch (start us, length us, event | category | flops | bytes accessed | tf_op | source)
XLA Modules:
  0.0 37.4 jit_solution(9152067689187064525)
XLA Ops:
  0.6 35.3 %exchange.1 = (bf16[128,32,256]{2,1,0:T(8,128)(2,1)S(1)}, f32[8,8192]{1,0:T(8,128)S(1)}) custom-call(bf16[128,32,256]{2,1,0:T(8,128)(2,1)} %bitcast.3, bf16[4,128,256]{2,1,0:T(8,128)(2,1)} %up_key.1, bf16[4,128,256]{2,1,0:T(8,128)(2,1)} %up_value.1, bf16[8,64,128]{2,1,0:T(8,128)(2,1)} %queries.1, s32[8]{0:T(128)} %lengths.1, s32[32,128]{1,0:T(8,128)} %bitcast.4), custom_call_target="tpu_custom_call" | custom-call | tf_op jit(solution)/shard_map/exchange/pallas_call | solution.py:288
  36.0 1.4 %store.1 = (bf16[128,32,256]{2,1,0:T(8,128)(2,1)}, f32[8,8192]{1,0:T(8,128)}) custom-call(bf16[128,32,256]{2,1,0:T(8,128)(2,1)S(1)} %get-tuple-element.6.received, f32[8,8192]{1,0:T(8,128)S(1)} %get-tuple-element.7.attended), custom_call_target="tpu_custom_call" | custom-call | tf_op jit(solution)/shard_map/store/pallas_call | solution.py:314

commit v5 on v4

--- a/solution.py
+++ b/solution.py
@@ -110,8 +110,8 @@
     dest_copy = pltpu.make_async_copy(block_dest.at[pl.ds(shard, 1)], dest_row, small_sem.at[0])
     dest_copy.start()
     lat_copy = pltpu.make_async_copy(latent, lat, lat_sem)
-    piece = blocks // 8
-    for k in range(8):
+    piece = blocks // 32
+    for k in range(32):
         part = pl.ds(k * piece, piece)
         pltpu.make_async_copy(latent.at[part], lat.at[part], lat_sem).start()
     small = [
@@ -193,8 +193,8 @@
         vals = lat[i * chunk_blocks : (i + 1) * chunk_blocks, :, rank : 2 * rank].reshape(width, rank)
         acc = acc + lax.dot_general(jnp.concatenate([hi, low], 0), vals, NN, preferred_element_type=F32)
     part_own[0:16] = acc[0:16] + acc[16:32]
-    part_own[16:32] = jnp.broadcast_to(top, (16, 128))
-    part_own[32:48] = jnp.broadcast_to(jnp.sum(total, axis=1, keepdims=True), (16, 128))
+    sums = jnp.sum(total, axis=1, keepdims=True)
+    part_own[16:32] = jnp.where(lax.broadcasted_iota(jnp.int32, (16, 128), 1) < 64, top, sums)
     part_all[quads] = part_own[...]
 
     pl.semaphore_wait(in_x, nx - 1)
@@ -214,13 +214,13 @@
 
     three = part_all.at[pl.ds(0, 3)]
     pltpu.make_async_copy(three, three, part_recv).wait()
-    tops = [part_all[k, 16:32] for k in range(4)]
+    tops = [part_all[k, 16:32, 0:1] for k in range(4)]
     top = jnp.maximum(jnp.maximum(tops[0], tops[1]), jnp.maximum(tops[2], tops[3]))
-    total = jnp.zeros((16, 128), F32)
+    total = jnp.zeros((16, 1), F32)
     acc = jnp.zeros((16, 128), F32)
     for k in range(4):
         factor = jnp.exp2(tops[k] - top)
-        total = total + part_all[k, 32:48] * factor
+        total = total + part_all[k, 16:32, 64:65] * factor
         acc = acc + part_all[k, 0:16] * factor
     mean = acc / total
     r0 = split_dot(mean[0:8], value_map[:, 0:head_dim], NN)
@@ -301,8 +301,8 @@
             pltpu.SMEM((1, blocks), jnp.int32),
             pltpu.SMEM((batch,), jnp.int32),
             pltpu.VMEM((16, blocks * tokens), F32),
-            pltpu.VMEM((48, 128), F32),
-            pltpu.VMEM((4, 48, 128), F32),
+            pltpu.VMEM((32, 128), F32),
+            pltpu.VMEM((4, 32, 128), F32),
             pltpu.VMEM((16, 128), F32),
             pltpu.VMEM((groups * batch, 16, 128), F32),
             dma, dma((5,)), dma, dma, dma, dma, dma, dma, dma, dma, dma,

time: 38 us -> 38.2 us (level)
  no operation moved by 1% of the time
where the time goes in v5:
time: 38.2 us; the launch traced here: 37.5 us
  Pallas kernels  36.9 us (97%)
  between operations  0.64 us (2%)
    pallas_call x1, Pallas kernels, body(): pl.pallas_call(functools.partial(exchange_kernel, sizes), out_shape=(pltp...  35.5 us
    pallas_call x1, Pallas kernels, body(): pl.pallas_call(store_kernel, out_shape=(jax.ShapeDtypeStruct((blocks, tok...  1.41 us

profile of v5, /device:TPU:0, one launch (start us, length us, event | category | flops | bytes accessed | tf_op | source)
XLA Modules:
  0.0 37.5 jit_solution(2909221651210106483)
XLA Ops:
  0.6 35.5 %exchange.1 = (bf16[128,32,256]{2,1,0:T(8,128)(2,1)S(1)}, f32[8,8192]{1,0:T(8,128)S(1)}) custom-call(bf16[128,32,256]{2,1,0:T(8,128)(2,1)} %bitcast.3, bf16[4,128,256]{2,1,0:T(8,128)(2,1)} %up_key.1, bf16[4,128,256]{2,1,0:T(8,128)(2,1)} %up_value.1, bf16[8,64,128]{2,1,0:T(8,128)(2,1)} %queries.1, s32[8]{0:T(128)} %lengths.1, s32[32,128]{1,0:T(8,128)} %bitcast.4), custom_call_target="tpu_custom_call" | custom-call | tf_op jit(solution)/shard_map/exchange/pallas_call | solution.py:288
  36.1 1.4 %store.1 = (bf16[128,32,256]{2,1,0:T(8,128)(2,1)}, f32[8,8192]{1,0:T(8,128)}) custom-call(bf16[128,32,256]{2,1,0:T(8,128)(2,1)S(1)} %get-tuple-element.6.received, f32[8,8192]{1,0:T(8,128)S(1)} %get-tuple-element.7.attended), custom_call_target="tpu_custom_call" | custom-call | tf_op jit(solution)/shard_map/store/pallas_call | solution.py:314

commit v6 on v4

--- a/solution.py
+++ b/solution.py
@@ -228,7 +228,7 @@
     result[0:8] = r0
     result[8:16] = r1
 
-    send_blocks(cube[:6])
+    send_blocks(cube[:20])
 
     half = y // 2
     slot = half * (nx * nz) + x * nz + z
@@ -239,7 +239,7 @@
             device_id=((z + dz) % nz, (x + dx) % nx, dest_y, 1 - c), device_id_type=MESH,
         ).start()
 
-    send_blocks(cube[6:])
+    send_blocks(cube[20:])
 
     per_half = nx * nz
     mine = c * half + (1 - c) * (1 - half)

time: 38 us -> 38.1 us (level)
  no operation moved by 1% of the time
where the time goes in v6:
time: 38.1 us; the launch traced here: 37.4 us
  Pallas kernels  36.7 us (96%)
  between operations  0.64 us (2%)
    pallas_call x1, Pallas kernels, body(): pl.pallas_call(functools.partial(exchange_kernel, sizes), out_shape=(pltp...  35.3 us
    pallas_call x1, Pallas kernels, body(): pl.pallas_call(store_kernel, out_shape=(jax.ShapeDtypeStruct((blocks, tok...  1.41 us

profile of v6, /device:TPU:0, one launch (start us, length us, event | category | flops | bytes accessed | tf_op | source)
XLA Modules:
  0.0 37.4 jit_solution(12421545599816222331)
XLA Ops:
  0.6 35.3 %exchange.1 = (bf16[128,32,256]{2,1,0:T(8,128)(2,1)S(1)}, f32[8,8192]{1,0:T(8,128)S(1)}) custom-call(bf16[128,32,256]{2,1,0:T(8,128)(2,1)} %bitcast.3, bf16[4,128,256]{2,1,0:T(8,128)(2,1)} %up_key.1, bf16[4,128,256]{2,1,0:T(8,128)(2,1)} %up_value.1, bf16[8,64,128]{2,1,0:T(8,128)(2,1)} %queries.1, s32[8]{0:T(128)} %lengths.1, s32[32,128]{1,0:T(8,128)} %bitcast.4), custom_call_target="tpu_custom_call" | custom-call | tf_op jit(solution)/shard_map/exchange/pallas_call | solution.py:288
  36.0 1.4 %store.1 = (bf16[128,32,256]{2,1,0:T(8,128)(2,1)}, f32[8,8192]{1,0:T(8,128)}) custom-call(bf16[128,32,256]{2,1,0:T(8,128)(2,1)S(1)} %get-tuple-element.6.received, f32[8,8192]{1,0:T(8,128)S(1)} %get-tuple-element.7.attended), custom_call_target="tpu_custom_call" | custom-call | tf_op jit(solution)/shard_map/store/pallas_call | solution.py:314
